TPU v7x, 512 devices: a whole 4x8x8 slice. The times are simulated.
512 devices in a mesh: bank: 32 (over y, x), zero: 16 (over z, core).
Axes of the slice: x: 4, y: 8, z: 8, core: 2. Of those that a mesh axis runs over, the one named last changes fastest.
Arguments:
- master_down: float32 [64, 1024, 2048], P('bank', None, 'zero'), may hold values from -0.25 to 0.25
- router_weight: float32 [2048, 64], P('zero', 'bank'), may hold values from -0.125 to 0.125
- router_gain: float32 [2048], P('zero'), may hold values from 0.25 to 1.75
Outputs:
- final_down: bfloat16 [64, 1024, 2048], P('bank')
- scale_down: float32 [64, 1024], P('bank')
- serve_router: bfloat16 [2048, 64], replicated
All inputs are finite; a program needn't handle non-finite values. Where the computation divides by a largest or mean magnitude, that divisor is 1e-20 or more.
Results may differ from a plain program's by a relative error of at most 0.001.
Values may be sent and summed in bfloat16 or wider, within the bound.
A program may use at most 64 MiB of HBM per device.

v0:
```python
import jax
import jax.numpy as jnp
from jax import lax
from jax.sharding import PartitionSpec as P


def copy_for_each(array, axis):
    count = lax.axis_size(axis)
    return lax.all_to_all(
        jnp.broadcast_to(array[None], (count, *array.shape)), axis, 0, 0, tiled=True
    )


def of_everyone(array, axis):
    return copy_for_each(array, axis).max(axis=0)


def joined_along(pieces, dim):
    pieces = jnp.moveaxis(pieces, 0, dim)
    shape = pieces.shape
    return pieces.reshape(*shape[:dim], shape[dim] * shape[dim + 1], *shape[dim + 2 :])


def collect(array, axis, dim):
    return joined_along(copy_for_each(array, axis), dim)


def per_device(master_down, router_weight, router_gain):
    scale_down = of_everyone(jnp.max(jnp.abs(master_down), axis=2), "zero")
    narrow_down = (master_down / jnp.expand_dims(scale_down, 2)).astype(jnp.bfloat16)
    final_down = lax.all_gather(narrow_down, "zero", axis=2, tiled=True)
    part_router = (router_weight * router_gain[:, None]).astype(jnp.bfloat16)
    row_router = lax.all_gather(part_router, "zero", axis=0, tiled=True)
    serve_router = collect(row_router, "bank", 1)
    return (final_down, scale_down, serve_router)


def solution(mesh):
    placed = (P("bank", None, "zero"), P("zero", "bank"), P("zero"))
    return jax.shard_map(
        per_device,
        mesh=mesh,
        in_specs=placed,
        out_specs=(P("bank", None, None), P("bank", None), P()),
        check_vma=False,
    )
```

profile of v0, /device:TPU:1, one launch (start us, length us, event | category | flops | bytes accessed | tf_op | source)
XLA Modules:
  0.0 114.2 jit_solution(8607611359955756124)
XLA Ops:
  7.2 0.0 all-gather.2.cloned.1.call-start
  7.2 1.6 %abs_reduce_fusion = f32[2,1024]{1,0:T(2,128)S(1)} fusion(f32[2,1024,128]{2,1,0:T(8,128)} %param.3), kind=kLoop, calls=%fused_computation.1 | loop fusion | flops 522240 | bytes 1056768 | tf_op jit(solution)/shard_map/reduce_max | solution.py:29
  8.8 20.5 %all_to_all.10 = f32[16,2,1024]{2,1,0:T(2,128)S(1)} all-to-all(f32[16,2,1024]{2,1,0:T(2,128)S(1)} %broadcast_in_dim.4), channel_id=1, replica_groups=mesh['bank'=32,'zero'=16] {'zero'}, dimensions={0} | all-to-all | bytes 262144 | tf_op jit(solution)/shard_map/all_to_all | solution.py:9
  29.3 0.1 reduce_max.19
  29.4 0.0 copy-start
  29.4 2.4 %divide_convert_fusion = bf16[2,1024,128]{2,1,0:T(8,128)(2,1)} fusion(f32[2,1024,128]{2,1,0:T(8,128)} %param.3, f32[2,1024]{1,0:T(2,128)S(1)} %reduce_max.19), kind=kLoop, calls=%fused_computation | loop fusion | flops 524288 | bytes 1581056 | tf_op jit(solution)/shard_map/convert_element_type | solution.py:30
  31.8 0.0 all-gather.2.cloned.1.call-update
  31.8 0.7 multiply_convert_fusion
  32.5 14.5 %all_gather.7 = bf16[2048,2]{0,1:T(2,128)(2,1)S(1)} all-gather(bf16[128,2]{0,1:T(2,128)(2,1)S(1)} %multiply_convert_fusion), channel_id=1, replica_groups=mesh['bank'=32,'zero'=16] {'zero'}, dimensions={0}, use_global_device_ids=true | all-gather | bytes 8704 | tf_op jit(solution)/shard_map/all_gather | solution.py:33
  46.9 0.1 broadcast_in_dim.5
  47.1 21.1 %all_to_all.11 = bf16[32,2048,2]{1,2,0:T(2,128)(2,1)S(1)} all-to-all(bf16[32,2048,2]{1,2,0:T(2,128)(2,1)S(1)} %broadcast_in_dim.5), channel_id=1, replica_groups=mesh['bank'=32,'zero'=16] {'bank'}, dimensions={0} | all-to-all | bytes 524288 | tf_op jit(solution)/shard_map/all_to_all | solution.py:9
  68.2 0.8 reshape.13
  69.0 29.9 %all-gather.2.cloned.1.call-done = bf16[2,1024,2048]{2,1,0:T(8,128)(2,1)} async-done(((bf16[2,1024,128]{2,1,0:T(8,128)(2,1)}), bf16[2,1024,2048]{2,1,0:T(8,128)(2,1)}) %all-gather.2.cloned.1.call-update) | async-done | bytes 8388624 | tf_op jit(solution)/shard_map/all_gather | solution.py:31
  98.9 8.4 %copy.9 = bf16[2,1024,2048]{2,1,0:T(8,128)(2,1)} copy(bf16[2,1024,2048]{2,1,0:T(8,128)(2,1)} %all-gather.2.cloned.1.call-done) | data formatting | bytes 16777216
  107.3 0.0 copy-done
  (1 shorter events, 0.0 us)
Async XLA Ops:
  7.2 91.7 %all-gather.2.cloned.1.call-start = ((), (), s32[]{:S(2)}) async-start(), calls=%async_computation.2 | async-start | bytes 8912896 | tf_op jit(solution)/shard_map/all_gather | solution.py:31
  29.4 77.9 %copy-start = (f32[2,1024]{1,0:T(2,128)}, f32[2,1024]{1,0:T(2,128)S(1)}, u32[]{:S(2)}) copy-start(f32[2,1024]{1,0:T(2,128)S(1)} %reduce_max.19) | copy-start | bytes 24580
Sparse Core Ops, SparseCore 0:
  31.9 66.9 all-gather.1
where the time goes:
time: 114 us
  blocking collectives  56.1 us (49%)
  waiting for transfers between devices  29.9 us (26%)
  between operations  14.1 us (12%)
  local copies, waits for them, and re-layouts  9.42 us (8%)
  other arithmetic  4.68 us (4%)
    all_to_all x2, blocking collectives, copy_for_each(): lax.all_to_all(jnp.broadcast_to(array[None], (count, *array.shape)), axis...  41.6 us
    all_gather x1, waiting for transfers between devices, per_device(): final_down = lax.all_gather(narrow_down, 'zero', axis=2, tiled=True)  29.9 us
    all_gather x1, blocking collectives, per_device(): row_router = lax.all_gather(part_router, 'zero', axis=0, tiled=True)  14.5 us
    unnamed x3, local copies, waits for them, and re-layouts  8.44 us
    convert_element_type x1, other arithmetic, per_device(): (master_down / jnp.expand_dims(scale_down, 2)).astype(jnp.bfloat16)  2.36 us
  transfers between devices with their start and end apart: 1, of which 1 were waited for; matrix products, arithmetic and copies ran while one was open for 1% of the time, Pallas kernels for 0%

commit v1 on v0

v1 whole, which is shorter than its diff:
```python
import functools

import jax
import jax.numpy as jnp
from jax import lax
from jax.experimental import pallas as pl
from jax.experimental.pallas import tpu as pltpu
from jax.sharding import PartitionSpec as P

MESH = pl.DeviceIdType.MESH
LANES = 128
CHUNK = 256
LOADS = 4
PUTS = 8


def kernel(
    banks, zeros, w_hbm, r_hbm, g_hbm, out, scale, router,
    w, r, g, maxima, rows, parts, columns,
    load_sem, max_send, max_recv, part_send, part_recv, col_send, col_recv,
    ring_send, ring_recv, pair_send, pair_recv,
):
    total = w_hbm.shape[0]
    chunks, blocks = total // CHUNK, total // LANES
    chips = zeros // 2
    half = chunks // 2
    bank, zero = lax.axis_index("bank"), lax.axis_index("zero")
    chip, core = zero // 2, lax.rem(zero, 2)
    partner = chip * 2 + 1 - core

    def shard_of(distance):
        return lax.rem(chip + distance + chips, chips) * 2 + core

    right, left = shard_of(1), shard_of(-1)

    barrier = pltpu.get_barrier_semaphore()
    share = total // LOADS

    def load(i):
        at = pl.ds(i * share, share)
        return pltpu.make_async_copy(w_hbm.at[at], w.at[at], load_sem.at[i])

    load_r = pltpu.make_async_copy(r_hbm, r, load_sem.at[LOADS])
    load_g = pltpu.make_async_copy(g_hbm, g, load_sem.at[LOADS + 1])
    for i in range(LOADS):
        load(i).start()
    load_r.start()
    load_g.start()

    @pl.loop(1, zeros)
    def _(d):
        pl.semaphore_signal(
            barrier, inc=1, device_id={"zero": lax.rem(zero + d, zeros)}, device_id_type=MESH
        )

    @pl.loop(1, banks)
    def _(d):
        pl.semaphore_signal(
            barrier, inc=1, device_id={"bank": lax.rem(bank + d, banks)}, device_id_type=MESH
        )

    for i in range(LOADS):
        load(i).wait()
        for j in range(i * blocks // LOADS, (i + 1) * blocks // LOADS):
            block = jnp.abs(w[j * LANES : (j + 1) * LANES, :])
            maxima[zero, j : j + 1, :] = jnp.max(block.T, axis=0, keepdims=True)
    load_r.wait()
    load_g.wait()
    product = r[...] * g[...]
    parts[zero, :, 0:LANES] = product[0:1]
    parts[zero, :, LANES : 2 * LANES] = product[1:2]

    pl.semaphore_wait(barrier, zeros - 1 + banks - 1)

    def send_max(peer):
        return pltpu.make_async_remote_copy(
            src_ref=maxima.at[zero], dst_ref=maxima.at[zero],
            send_sem=max_send.at[peer], recv_sem=max_recv.at[zero],
            device_id={"zero": peer}, device_id_type=MESH,
        )

    def take_max(peer):
        return pltpu.make_async_remote_copy(
            src_ref=maxima.at[peer], dst_ref=maxima.at[peer],
            send_sem=max_send.at[peer], recv_sem=max_recv.at[peer],
            device_id={"zero": peer}, device_id_type=MESH,
        )

    def send_part(peer):
        return pltpu.make_async_remote_copy(
            src_ref=parts.at[zero], dst_ref=parts.at[zero],
            send_sem=part_send.at[peer], recv_sem=part_recv.at[zero],
            device_id={"zero": peer}, device_id_type=MESH,
        )

    def take_part(peer):
        return pltpu.make_async_remote_copy(
            src_ref=parts.at[peer], dst_ref=parts.at[peer],
            send_sem=part_send.at[peer], recv_sem=part_recv.at[peer],
            device_id={"zero": peer}, device_id_type=MESH,
        )

    offsets = sorted(range(1, chips), key=lambda o: -min(o, chips - o))
    peers = [lax.rem(chip + o, chips) * 2 + c for o in offsets for c in (core, 1 - core)]
    peers.append(partner)
    for peer in peers:
        send_max(peer).start()
    for peer in peers:
        send_part(peer).start()
    for peer in reversed(peers):
        take_max(peer).wait_recv()

    most = maxima[0]
    for i in range(1, zeros):
        most = jnp.maximum(most, maxima[i])
    rows[...] = most
    half_blocks = blocks // 2
    for j in range(blocks):
        e, at = j // half_blocks, (j % half_blocks) * LANES
        scale[e : e + 1, at : at + LANES] = most[j : j + 1, :]

    def piece(shard, k):
        return out.at[
            pl.ds(pl.multiple_of(k * CHUNK, CHUNK), CHUNK),
            pl.ds(pl.multiple_of(shard * LANES, LANES), LANES),
        ]

    def hop(way, step, shard, k):
        return pltpu.make_async_remote_copy(
            src_ref=piece(shard, k), dst_ref=piece(shard, k),
            send_sem=ring_send.at[way, step, k], recv_sem=ring_recv.at[way, step, k],
            device_id={"zero": (right, left)[way]}, device_id_type=MESH,
        )

    def pair(slot, shard, k):
        return pltpu.make_async_remote_copy(
            src_ref=piece(shard, k), dst_ref=piece(shard, k),
            send_sem=pair_send.at[slot, k], recv_sem=pair_recv.at[slot, k],
            device_id={"zero": partner}, device_id_type=MESH,
        )

    @pl.loop(0, chunks)
    def _(k):
        for i in range(CHUNK // LANES):
            j = k * (CHUNK // LANES) + i
            at = pl.ds(pl.multiple_of(j * LANES, LANES), LANES)
            by = jnp.broadcast_to(rows[pl.ds(j, 1), :], (LANES, LANES)).T
            to = pl.ds(pl.multiple_of(zero * LANES, LANES), LANES)
            out[at, to] = (w[at, :] / by).astype(jnp.bfloat16)
        hop(0, 0, zero, k).start()
        hop(1, 0, zero, k).start()
        pair(0, zero, k).start()

    for peer in peers:
        take_part(peer).wait_recv()
    tile = pl.multiple_of(bank * 2 * zeros, 2 * zeros)
    for i in range(zeros):
        columns[pl.ds(tile + i, 1), :] = parts[i, :, 0:LANES]
        columns[pl.ds(tile + zeros + i, 1), :] = parts[i, :, LANES : 2 * LANES]

    def column_copy(owner, peer):
        at = pl.ds(pl.multiple_of(owner * 2 * zeros, 2 * zeros), 2 * zeros)
        return pltpu.make_async_remote_copy(
            src_ref=columns.at[at], dst_ref=columns.at[at],
            send_sem=col_send.at[peer], recv_sem=col_recv.at[owner],
            device_id={"bank": peer}, device_id_type=MESH,
        )

    @pl.loop(1, banks)
    def _(d):
        column_copy(bank, lax.rem(bank + d, banks)).start()

    def forward(way, step, k, onward):
        distance = -step if way == 0 else step
        shard = shard_of(distance)
        slot = distance % chips
        hop(way, step - 1, shard, k).wait_recv()
        if onward:
            hop(way, step, shard, k).start()
        pair(slot, shard, k).start()

    def finish_router():
        @pl.loop(1, banks)
        def _(d):
            owner = lax.rem(bank + d, banks)
            column_copy(owner, owner).wait_recv()

        for i in range(zeros):
            router[:, i * LANES : (i + 1) * LANES] = columns[
                pl.ds(i, 2 * banks, stride=zeros), :
            ].astype(jnp.bfloat16)

    far = chips // 2
    for step in range(1, far):
        if step < far - 1:

            @pl.loop(0, chunks)
            def _(k):
                forward(0, step, k, True)
                forward(1, step, k, True)
        else:

            @pl.loop(0, half)
            def _(k):
                forward(0, step, k, True)
                forward(1, step, k, False)

            @pl.loop(half, chunks)
            def _(k):
                forward(0, step, k, False)
                forward(1, step, k, True)

        if step == far - 2:
            finish_router()

    @pl.loop(0, half)
    def _(k):
        forward(0, far, k, False)
        forward(1, far, k + half, False)

    for distance in range(chips):

        @pl.loop(0, chunks)
        def _(k):
            pair(distance, lax.rem(chip + distance, chips) * 2 + 1 - core, k).wait_recv()

        @pl.loop(0, chunks)
        def _(k):
            pair(distance, shard_of(distance), k).wait_send()

    for step in range(far):
        for way in (0, 1):
            distance = -step if way == 0 else step
            first, last = 0, chunks
            if step == far - 1:
                first, last = (0, half) if way == 0 else (half, chunks)

            @pl.loop(first, last)
            def _(k):
                hop(way, step, shard_of(distance), k).wait_send()

    for peer in peers:
        send_max(peer).wait_send()
        send_part(peer).wait_send()

    @pl.loop(1, banks)
    def _(d):
        column_copy(bank, lax.rem(bank + d, banks)).wait_send()


def put_out(final, scale, router, final_hbm, scale_hbm, router_hbm, sem):
    share = final.shape[0] // PUTS
    copies = [
        pltpu.make_async_copy(
            final.at[pl.ds(i * share, share)], final_hbm.at[pl.ds(i * share, share)], sem.at[i]
        )
        for i in range(PUTS)
    ]
    copies.append(pltpu.make_async_copy(scale, scale_hbm, sem.at[PUTS]))
    copies.append(pltpu.make_async_copy(router, router_hbm, sem.at[PUTS + 1]))
    for copy in copies:
        copy.start()
    for copy in copies:
        copy.wait()


def per_device(banks, zeros, master_down, router_weight, router_gain):
    experts, inner, width = master_down.shape
    total = experts * inner
    chunks, chips = total // CHUNK, zeros // 2
    dma = pltpu.SemaphoreType.DMA
    final, scale, router = pl.pallas_call(
        functools.partial(kernel, banks, zeros),
        out_shape=(
            jax.ShapeDtypeStruct((total, width * zeros), jnp.bfloat16),
            jax.ShapeDtypeStruct((experts, inner), jnp.float32),
            jax.ShapeDtypeStruct((2 * banks, LANES * zeros), jnp.bfloat16),
        ),
        in_specs=[pl.BlockSpec(memory_space=pltpu.HBM)] * 3,
        out_specs=(pl.BlockSpec(memory_space=pltpu.VMEM),) * 3,
        scratch_shapes=[
            pltpu.VMEM((total, LANES), jnp.float32),
            pltpu.VMEM((2, LANES), jnp.float32),
            pltpu.VMEM((1, LANES), jnp.float32),
            pltpu.VMEM((zeros, total // LANES, LANES), jnp.float32),
            pltpu.VMEM((total // LANES, LANES), jnp.float32),
            pltpu.VMEM((zeros, 1, 2 * LANES), jnp.float32),
            pltpu.VMEM((2 * banks * zeros, LANES), jnp.float32),
            dma((LOADS + 2,)),
            dma((zeros,)),
            dma((zeros,)),
            dma((zeros,)),
            dma((zeros,)),
            dma((banks,)),
            dma((banks,)),
            dma((2, chips // 2, chunks)),
            dma((2, chips // 2, chunks)),
            dma((chips, chunks)),
            dma((chips, chunks)),
        ],
        compiler_params=pltpu.CompilerParams(
            collective_id=0, has_side_effects=True, vmem_limit_bytes=24 * 1024 * 1024
        ),
    )(
        *(
            pltpu.with_memory_space_constraint(a, pltpu.HBM)
            for a in (
                master_down.reshape(total, width),
                router_weight.T,
                router_gain.reshape(1, LANES),
            )
        )
    )
    final, scale, router = pl.pallas_call(
        put_out,
        out_shape=tuple(jax.ShapeDtypeStruct(a.shape, a.dtype) for a in (final, scale, router)),
        in_specs=[pl.BlockSpec(memory_space=pltpu.VMEM)] * 3,
        out_specs=(pl.BlockSpec(memory_space=pltpu.HBM),) * 3,
        scratch_shapes=[dma((PUTS + 2,))],
        compiler_params=pltpu.CompilerParams(vmem_limit_bytes=1024 * 1024),
    )(final, scale, router)
    return final.reshape(experts, inner, width * zeros), scale, router.T


def solution(mesh):
    banks, zeros = mesh.shape["bank"], mesh.shape["zero"]
    return jax.shard_map(
        functools.partial(per_device, banks, zeros),
        mesh=mesh,
        in_specs=(P("bank", None, "zero"), P("zero", "bank"), P("zero")),
        out_specs=(P("bank", None, None), P("bank", None), P()),
        check_vma=False,
    )
```

time: 114 us -> 74.5 us (0.65)
  Pallas kernels: 0 us -> 73.7 us
  blocking collectives: 56.1 us -> 0 us
  waiting for transfers between devices: 29.9 us -> 0 us
  between operations: 14.1 us -> 0.64 us
  local copies, waits for them, and re-layouts: 9.42 us -> 0 us
  other arithmetic: 4.68 us -> 0 us
    pallas_call x0 -> x2, Pallas kernels: none -> 73.7 us  [the longest x1 70.3 us: per_device(): pl.pallas_call(functools.partial(kernel, banks, zeros), out_shape=(jax.Sh...]
    all_to_all x2 -> x0, blocking collectives: 41.6 us -> none  [copy_for_each(): lax.all_to_all(jnp.broadcast_to(array[None], (count, *array.shape)), axis...]
    all_gather x1 -> x0, waiting for transfers between devices: 29.9 us -> none  [per_device(): final_down = lax.all_gather(narrow_down, 'zero', axis=2, tiled=True)]
    all_gather x1 -> x0, blocking collectives: 14.5 us -> none  [per_device(): row_router = lax.all_gather(part_router, 'zero', axis=0, tiled=True)]
    unnamed x3 -> x0, local copies, waits for them, and re-layouts: 8.44 us -> none
    convert_element_type x2 -> x0, other arithmetic: 3.05 us -> none  [the longest x1 2.36 us: per_device(): (master_down / jnp.expand_dims(scale_down, 2)).astype(jnp.bfloat16)]
    reduce_max x2 -> x0, other arithmetic: 1.63 us -> none  [the longest x1 1.57 us: per_device(): scale_down = of_everyone(jnp.max(jnp.abs(master_down), axis=2), 'zero')]
  transfers between devices with their start and end apart: 1 -> 0, of which waited for: 1 -> 0; matrix products, arithmetic and copies ran while one was open for 1% -> 0% of each run, Pallas kernels for 0% -> 0%
where the time goes in v1:
time: 74.5 us; the launch traced here: 74.4 us
  Pallas kernels  73.7 us (99%)
    pallas_call x1, Pallas kernels, per_device(): pl.pallas_call(functools.partial(kernel, banks, zeros), out_shape=(jax.Sh...  70.3 us
    pallas_call x1, Pallas kernels, per_device(): pl.pallas_call(put_out, out_shape=tuple((jax.ShapeDtypeStruct(a.shape, a....  3.44 us

profile of v1, /device:TPU:1, one launch (start us, length us, event | category | flops | bytes accessed | tf_op | source)
XLA Modules:
  0.0 74.4 jit_solution(7837891572347357455)
XLA Ops:
  0.6 70.3 %shard_map.58 = (bf16[2048,2048]{1,0:T(8,128)(2,1)S(1)}, f32[2,1024]{1,0:T(2,128)S(1)}, bf16[64,2048]{1,0:T(8,128)(2,1)S(1)}) custom-call(f32[2048,128]{1,0:T(8,128)} %bitcast.5, f32[2,128]{1,0:T(2,128)} %bitcast.6, f32[1,128]{1,0:T(1,128)} %bitcast.7), custom_call_target="tpu_custom_call" | custom-call | tf_op jit(solution)/shard_map/pallas_call | solution.py:272
  70.9 3.4 %shard_map.59 = (bf16[2048,2048]{1,0:T(8,128)(2,1)}, f32[2,1024]{1,0:T(2,128)}, bf16[64,2048]{1,0:T(8,128)(2,1)}) custom-call(bf16[2048,2048]{1,0:T(8,128)(2,1)S(1)} %get-tuple-element.9.final, f32[2,1024]{1,0:T(2,128)S(1)} %get-tuple-element.10.scale, bf16[64,2048]{1,0:T(8,128)(2,1)S(1)} %get-tuple-element.11.router), custom_call_target="tpu_custom_call" | custom-call | tf_op jit(solution)/shard_map/pallas_call | solution.py:314

commit v2 on v0

v2 whole, which is shorter than its diff:
```python
import functools

import jax
import jax.numpy as jnp
from jax import lax
from jax.experimental import pallas as pl
from jax.experimental.pallas import tpu as pltpu
from jax.sharding import PartitionSpec as P

MESH = pl.DeviceIdType.MESH
LANES = 128
ACROSS = 4
CHUNKS = 4
PUTS = 8
ORDER = ((0, 1, 2, 3), (1, 0, 3, 2))
ONWARD = ((0, 2), (1, 3))


def kernel(
    banks, zeros, w_hbm, r_hbm, g_hbm, out, scale, router,
    w, r, g, maxima, rows, parts, columns,
    load_sem, max_send, max_recv, part_send, part_recv, col_send, x_recv, y_recv,
    ring_send, ring_recv, pair_send, pair_recv,
):
    total = w_hbm.shape[0]
    chunk, blocks = total // CHUNKS, total // LANES
    half_blocks = blocks // 2
    chips, down = zeros // 2, banks // ACROSS
    far = chips // 2
    bank, zero = lax.axis_index("bank"), lax.axis_index("zero")
    chip, core = zero // 2, lax.rem(zero, 2)
    partner = chip * 2 + 1 - core
    y, x = bank // ACROSS, lax.rem(bank, ACROSS)

    def shard_of(distance):
        return lax.rem(chip + distance + chips, chips) * 2 + core

    def along_x(distance):
        return y * ACROSS + lax.rem(x + distance + ACROSS, ACROSS)

    def along_y(distance):
        return lax.rem(y + distance + down, down)

    def remote(src, dst, send_sem, recv_sem, **device):
        return pltpu.make_async_remote_copy(
            src_ref=src, dst_ref=dst, send_sem=send_sem, recv_sem=recv_sem,
            device_id=device, device_id_type=MESH,
        )

    offsets = sorted(range(1, chips), key=lambda o: -min(o, chips - o))
    peers = [lax.rem(chip + o, chips) * 2 + c for o in offsets for c in (core, 1 - core)]
    peers.append(partner)
    barrier = pltpu.get_barrier_semaphore()
    for peer in peers:
        pl.semaphore_signal(barrier, inc=1, device_id={"zero": peer}, device_id_type=MESH)

    def load(i):
        at = pl.ds(i * chunk, chunk)
        return pltpu.make_async_copy(w_hbm.at[at], w.at[at], load_sem.at[i])

    load_r = pltpu.make_async_copy(r_hbm, r, load_sem.at[CHUNKS])
    load_g = pltpu.make_async_copy(g_hbm, g, load_sem.at[CHUNKS + 1])
    for i in range(CHUNKS):
        load(i).start()
    load_r.start()
    load_g.start()
    beside = [along_x(1), along_x(-1), along_y(1) * ACROSS + x]
    if down > 2:
        beside.append(along_y(-1) * ACROSS + x)
    for peer in beside:
        pl.semaphore_signal(barrier, inc=1, device_id={"bank": peer}, device_id_type=MESH)

    for i in range(CHUNKS):
        load(i).wait()
        for j in range(i * blocks // CHUNKS, (i + 1) * blocks // CHUNKS):
            block = jnp.abs(w[j * LANES : (j + 1) * LANES, :])
            h, k = j // half_blocks, j % half_blocks
            maxima[h, zero, k : k + 1, :] = jnp.max(block.T, axis=0, keepdims=True)
    load_r.wait()
    load_g.wait()
    product = r[...] * g[...]
    parts[zero, :, 0:LANES] = product[0:1]
    parts[zero, :, LANES : 2 * LANES] = product[1:2]

    pl.semaphore_wait(barrier, zeros - 1 + len(beside))

    for h in (0, 1):
        for peer in peers:
            mine = maxima.at[h, zero]
            remote(mine, mine, max_send.at[h], max_recv.at[h], zero=peer).start()
    for peer in peers:
        mine = parts.at[zero]
        remote(mine, mine, part_send.at[0], part_recv.at[0], zero=peer).start()

    right, left = shard_of(1), shard_of(-1)

    def piece(shard, k):
        return out.at[
            pl.ds(k * chunk, chunk), pl.ds(pl.multiple_of(shard * LANES, LANES), LANES)
        ]

    def hop(way, step, shard, k):
        at = piece(shard, k)
        return remote(
            at, at, ring_send.at[0], ring_recv.at[way, step, k], zero=(right, left)[way]
        )

    def pair(shard, k):
        at = piece(shard, k)
        return remote(at, at, pair_send.at[0], pair_recv.at[0], zero=partner)

    def divide(k):
        for j in range(k * blocks // CHUNKS, (k + 1) * blocks // CHUNKS):
            at = pl.ds(j * LANES, LANES)
            by = jnp.broadcast_to(rows[j : j + 1, :], (LANES, LANES)).T
            to = pl.ds(pl.multiple_of(zero * LANES, LANES), LANES)
            out[at, to] = (w[at, :] / by).astype(jnp.bfloat16)

    for h in (0, 1):
        others = maxima.at[h, pl.ds(0, zeros - 1)]
        remote(others, others, max_send.at[h], max_recv.at[h], zero=partner).wait_recv()
        most = maxima[h, 0]
        for i in range(1, zeros):
            most = jnp.maximum(most, maxima[h, i])
        rows[h * half_blocks : (h + 1) * half_blocks, :] = most
        first, second = 2 * h, 2 * h + 1
        divide(first)
        hop(0, 0, zero, first).start()
        divide(second)
        hop(1, 0, zero, second).start()
        hop(0, 0, zero, second).start()
        hop(1, 0, zero, first).start()
        pair(zero, first).start()
        pair(zero, second).start()

    per_expert = blocks // scale.shape[0]
    for j in range(blocks):
        e, at = j // per_expert, (j % per_expert) * LANES
        scale[e : e + 1, at : at + LANES] = rows[j : j + 1, :]

    def banks_of(first, count):
        size = count * 2 * zeros
        return columns.at[pl.ds(pl.multiple_of(first * 2 * zeros, 2 * zeros), size)]

    def send_x(distance, peer):
        at = banks_of(along_x(distance), 1)
        return remote(at, at, col_send.at[0], x_recv.at[distance % ACROSS], bank=peer)

    def send_y(distance, peer):
        at = banks_of(along_y(distance) * ACROSS, ACROSS)
        return remote(
            at, at, col_send.at[0], y_recv.at[distance % down], bank=peer * ACROSS + x
        )

    def x_first():
        others = parts.at[pl.ds(0, zeros - 1)]
        remote(others, others, part_send.at[0], part_recv.at[0], zero=partner).wait_recv()
        tile = pl.multiple_of(bank * 2 * zeros, 2 * zeros)
        for i in range(zeros):
            columns[pl.ds(tile + i, 1), :] = parts[i, :, 0:LANES]
            columns[pl.ds(tile + zeros + i, 1), :] = parts[i, :, LANES : 2 * LANES]
        at = banks_of(bank, 1)
        remote(at, at, col_send.at[0], x_recv.at[ACROSS - 1], bank=along_x(1)).start()
        remote(at, at, col_send.at[0], x_recv.at[1], bank=along_x(-1)).start()

    def x_second():
        send_x(-1, along_x(1)).wait_recv()
        send_x(1, along_x(-1)).wait_recv()
        at = banks_of(along_x(-1), 1)
        remote(at, at, col_send.at[0], x_recv.at[2], bank=along_x(1)).start()

    ups, downs = down // 2, (down - 1) // 2

    def y_step(step):
        if step == 0:
            send_x(2, along_x(1)).wait_recv()
        if 1 <= step <= ups:
            send_y(-step, along_y(1)).wait_recv()
        if 1 <= step <= downs:
            send_y(step, along_y(-1)).wait_recv()
        if step < ups:
            at = banks_of(along_y(-step) * ACROSS, ACROSS)
            remote(
                at, at, col_send.at[0], y_recv.at[(-step - 1) % down],
                bank=along_y(1) * ACROSS + x,
            ).start()
        if step < downs:
            at = banks_of(along_y(step) * ACROSS, ACROSS)
            remote(
                at, at, col_send.at[0], y_recv.at[(step + 1) % down],
                bank=along_y(-1) * ACROSS + x,
            ).start()

    def finish_router():
        for i in range(zeros):
            router[:, i * LANES : (i + 1) * LANES] = columns[
                pl.ds(i, 2 * banks, stride=zeros), :
            ].astype(jnp.bfloat16)

    stages = [x_second] + [functools.partial(y_step, step) for step in range(ups + 1)]

    def forward(way, step, k, onward):
        shard = shard_of(-step if way == 0 else step)
        hop(way, step - 1, shard, k).wait_recv()
        if onward:
            hop(way, step, shard, k).start()
        pair(shard, k).start()

    x_first()
    for step in range(1, far):
        for i in range(CHUNKS):
            for way in (0, 1):
                k = ORDER[way][i]
                forward(way, step, k, step < far - 1 or k in ONWARD[way])
            if i % 2 == 1 and stages:
                stages.pop(0)()
    for stage in stages:
        stage()
    finish_router()
    for i in range(CHUNKS // 2):
        for way in (0, 1):
            forward(way, far, ONWARD[way][i], False)

    sent = out.at[:, pl.ds(0, (chips - 1) * LANES)]
    remote(sent, sent, ring_send.at[0], ring_recv.at[0, 0, 0], zero=right).wait_send()
    for h in (0, 1):
        others = maxima.at[h, pl.ds(0, zeros - 1)]
        remote(others, others, max_send.at[h], max_recv.at[h], zero=partner).wait_send()
    others = parts.at[pl.ds(0, zeros - 1)]
    remote(others, others, part_send.at[0], part_recv.at[0], zero=partner).wait_send()
    size = (ACROSS - 1 + (down - 1) * ACROSS) * 2 * zeros
    others = columns.at[pl.ds(0, size)]
    remote(others, others, col_send.at[0], x_recv.at[0], bank=along_x(1)).wait_send()
    both = out.at[:, pl.ds(0, chips * LANES)]
    remote(both, both, pair_send.at[0], pair_recv.at[0], zero=partner).wait()


def put_out(final, scale, router, final_hbm, scale_hbm, router_hbm, sem):
    share = final.shape[0] // PUTS
    copies = [
        pltpu.make_async_copy(
            final.at[pl.ds(i * share, share)], final_hbm.at[pl.ds(i * share, share)], sem.at[i]
        )
        for i in range(PUTS)
    ]
    copies.append(pltpu.make_async_copy(scale, scale_hbm, sem.at[PUTS]))
    copies.append(pltpu.make_async_copy(router, router_hbm, sem.at[PUTS + 1]))
    for copy in copies:
        copy.start()
    for copy in copies:
        copy.wait()


def per_device(banks, zeros, master_down, router_weight, router_gain):
    experts, inner, width = master_down.shape
    total = experts * inner
    chips = zeros // 2
    dma = pltpu.SemaphoreType.DMA
    final, scale, router = pl.pallas_call(
        functools.partial(kernel, banks, zeros),
        out_shape=(
            jax.ShapeDtypeStruct((total, width * zeros), jnp.bfloat16),
            jax.ShapeDtypeStruct((experts, inner), jnp.float32),
            jax.ShapeDtypeStruct((2 * banks, LANES * zeros), jnp.bfloat16),
        ),
        in_specs=[pl.BlockSpec(memory_space=pltpu.HBM)] * 3,
        out_specs=(pl.BlockSpec(memory_space=pltpu.VMEM),) * 3,
        scratch_shapes=[
            pltpu.VMEM((total, LANES), jnp.float32),
            pltpu.VMEM((2, LANES), jnp.float32),
            pltpu.VMEM((1, LANES), jnp.float32),
            pltpu.VMEM((2, zeros, total // LANES // 2, LANES), jnp.float32),
            pltpu.VMEM((total // LANES, LANES), jnp.float32),
            pltpu.VMEM((zeros, 1, 2 * LANES), jnp.float32),
            pltpu.VMEM((2 * banks * zeros, LANES), jnp.float32),
            dma((CHUNKS + 2,)),
            dma((2,)),
            dma((2,)),
            dma((1,)),
            dma((1,)),
            dma((1,)),
            dma((ACROSS,)),
            dma((banks // ACROSS,)),
            dma((1,)),
            dma((2, chips // 2, CHUNKS)),
            dma((1,)),
            dma((1,)),
        ],
        compiler_params=pltpu.CompilerParams(
            collective_id=0, has_side_effects=True, vmem_limit_bytes=24 * 1024 * 1024
        ),
    )(
        *(
            pltpu.with_memory_space_constraint(a, pltpu.HBM)
            for a in (
                master_down.reshape(total, width),
                router_weight.T,
                router_gain.reshape(1, LANES),
            )
        )
    )
    final, scale, router = pl.pallas_call(
        put_out,
        out_shape=tuple(jax.ShapeDtypeStruct(a.shape, a.dtype) for a in (final, scale, router)),
        in_specs=[pl.BlockSpec(memory_space=pltpu.VMEM)] * 3,
        out_specs=(pl.BlockSpec(memory_space=pltpu.HBM),) * 3,
        scratch_shapes=[dma((PUTS + 2,))],
        compiler_params=pltpu.CompilerParams(vmem_limit_bytes=1024 * 1024),
    )(final, scale, router)
    return final.reshape(experts, inner, width * zeros), scale, router.T


def solution(mesh):
    banks, zeros = mesh.shape["bank"], mesh.shape["zero"]
    return jax.shard_map(
        functools.partial(per_device, banks, zeros),
        mesh=mesh,
        in_specs=(P("bank", None, "zero"), P("zero", "bank"), P("zero")),
        out_specs=(P("bank", None, None), P("bank", None), P()),
        check_vma=False,
    )
```

time: 114 us -> 65.3 us (0.57)
  Pallas kernels: 0 us -> 64.5 us
  blocking collectives: 56.1 us -> 0 us
  waiting for transfers between devices: 29.9 us -> 0 us
  between operations: 14.1 us -> 0.64 us
  local copies, waits for them, and re-layouts: 9.42 us -> 0 us
  other arithmetic: 4.68 us -> 0 us
    pallas_call x0 -> x2, Pallas kernels: none -> 64.5 us  [the longest x1 61.1 us: per_device(): pl.pallas_call(functools.partial(kernel, banks, zeros), out_shape=(jax.Sh...]
    all_to_all x2 -> x0, blocking collectives: 41.6 us -> none  [copy_for_each(): lax.all_to_all(jnp.broadcast_to(array[None], (count, *array.shape)), axis...]
    all_gather x1 -> x0, waiting for transfers between devices: 29.9 us -> none  [per_device(): final_down = lax.all_gather(narrow_down, 'zero', axis=2, tiled=True)]
    all_gather x1 -> x0, blocking collectives: 14.5 us -> none  [per_device(): row_router = lax.all_gather(part_router, 'zero', axis=0, tiled=True)]
    unnamed x3 -> x0, local copies, waits for them, and re-layouts: 8.44 us -> none
    convert_element_type x2 -> x0, other arithmetic: 3.05 us -> none  [the longest x1 2.36 us: per_device(): (master_down / jnp.expand_dims(scale_down, 2)).astype(jnp.bfloat16)]
    reduce_max x2 -> x0, other arithmetic: 1.63 us -> none  [the longest x1 1.57 us: per_device(): scale_down = of_everyone(jnp.max(jnp.abs(master_down), axis=2), 'zero')]
  transfers between devices with their start and end apart: 1 -> 0, of which waited for: 1 -> 0; matrix products, arithmetic and copies ran while one was open for 1% -> 0% of each run, Pallas kernels for 0% -> 0%
where the time goes in v2:
time: 65.3 us; the launch traced here: 65.2 us
  Pallas kernels  64.5 us (99%)
    pallas_call x1, Pallas kernels, per_device(): pl.pallas_call(functools.partial(kernel, banks, zeros), out_shape=(jax.Sh...  61.1 us
    pallas_call x1, Pallas kernels, per_device(): pl.pallas_call(put_out, out_shape=tuple((jax.ShapeDtypeStruct(a.shape, a....  3.44 us

profile of v2, /device:TPU:1, one launch (start us, length us, event | category | flops | bytes accessed | tf_op | source)
XLA Modules:
  0.0 65.2 jit_solution(17104875505107197277)
XLA Ops:
  0.6 61.1 %shard_map.58 = (bf16[2048,2048]{1,0:T(8,128)(2,1)S(1)}, f32[2,1024]{1,0:T(2,128)S(1)}, bf16[64,2048]{1,0:T(8,128)(2,1)S(1)}) custom-call(f32[2048,128]{1,0:T(8,128)} %bitcast.5, f32[2,128]{1,0:T(2,128)} %bitcast.6, f32[1,128]{1,0:T(1,128)} %bitcast.7), custom_call_target="tpu_custom_call" | custom-call | tf_op jit(solution)/shard_map/pallas_call | solution.py:259
  61.7 3.4 %shard_map.59 = (bf16[2048,2048]{1,0:T(8,128)(2,1)}, f32[2,1024]{1,0:T(2,128)}, bf16[64,2048]{1,0:T(8,128)(2,1)}) custom-call(bf16[2048,2048]{1,0:T(8,128)(2,1)S(1)} %get-tuple-element.9.final, f32[2,1024]{1,0:T(2,128)S(1)} %get-tuple-element.10.scale, bf16[64,2048]{1,0:T(8,128)(2,1)S(1)} %get-tuple-element.11.router), custom_call_target="tpu_custom_call" | custom-call | tf_op jit(solution)/shard_map/pallas_call | solution.py:302

commit v3 on v2

--- a/solution.py
+++ b/solution.py
@@ -10,23 +10,36 @@
 MESH = pl.DeviceIdType.MESH
 LANES = 128
 ACROSS = 4
-CHUNKS = 4
+LOADS = 4
 PUTS = 8
-ORDER = ((0, 1, 2, 3), (1, 0, 3, 2))
-ONWARD = ((0, 2), (1, 3))
+PIECES = (4, 2, 2, 4, 4)
+EARLY = PIECES[0] * LANES
+ORDER = ((0, 1, 2, 3, 4), (0, 1, 3, 4, 2))
+ONWARD = ((0, 1, 2), (3, 4))
+
+
+def arrivals(chips):
+    keys = [
+        (way, step, k)
+        for way in (0, 1)
+        for step in range(chips // 2)
+        for k in range(len(PIECES))
+        if step < chips // 2 - 1 or k in ONWARD[way]
+    ]
+    return {key: i for i, key in enumerate(keys)}
 
 
 def kernel(
     banks, zeros, w_hbm, r_hbm, g_hbm, out, scale, router,
-    w, r, g, maxima, rows, parts, columns,
+    w, r, g, early, maxima, shared, rows, parts, columns,
     load_sem, max_send, max_recv, part_send, part_recv, col_send, x_recv, y_recv,
-    ring_send, ring_recv, pair_send, pair_recv,
+    early_send, ring_send, ring_recv, pair_send, pair_recv,
 ):
     total = w_hbm.shape[0]
-    chunk, blocks = total // CHUNKS, total // LANES
+    blocks = total // LANES
     half_blocks = blocks // 2
     chips, down = zeros // 2, banks // ACROSS
-    far = chips // 2
+    far, number = chips // 2, arrivals(chips)
     bank, zero = lax.axis_index("bank"), lax.axis_index("zero")
     chip, core = zero // 2, lax.rem(zero, 2)
     partner = chip * 2 + 1 - core
@@ -54,13 +67,15 @@
     for peer in peers:
         pl.semaphore_signal(barrier, inc=1, device_id={"zero": peer}, device_id_type=MESH)
 
+    share = total // LOADS
+
     def load(i):
-        at = pl.ds(i * chunk, chunk)
+        at = pl.ds(i * share, share)
         return pltpu.make_async_copy(w_hbm.at[at], w.at[at], load_sem.at[i])
 
-    load_r = pltpu.make_async_copy(r_hbm, r, load_sem.at[CHUNKS])
-    load_g = pltpu.make_async_copy(g_hbm, g, load_sem.at[CHUNKS + 1])
-    for i in range(CHUNKS):
+    load_r = pltpu.make_async_copy(r_hbm, r, load_sem.at[LOADS])
+    load_g = pltpu.make_async_copy(g_hbm, g, load_sem.at[LOADS + 1])
+    for i in range(LOADS):
         load(i).start()
     load_r.start()
     load_g.start()
@@ -70,9 +85,9 @@
     for peer in beside:
         pl.semaphore_signal(barrier, inc=1, device_id={"bank": peer}, device_id_type=MESH)
 
-    for i in range(CHUNKS):
+    for i in range(LOADS):
         load(i).wait()
-        for j in range(i * blocks // CHUNKS, (i + 1) * blocks // CHUNKS):
+        for j in range(i * blocks // LOADS, (i + 1) * blocks // LOADS):
             block = jnp.abs(w[j * LANES : (j + 1) * LANES, :])
             h, k = j // half_blocks, j % half_blocks
             maxima[h, zero, k : k + 1, :] = jnp.max(block.T, axis=0, keepdims=True)
@@ -84,54 +99,101 @@
 
     pl.semaphore_wait(barrier, zeros - 1 + len(beside))
 
-    for h in (0, 1):
-        for peer in peers:
-            mine = maxima.at[h, zero]
-            remote(mine, mine, max_send.at[h], max_recv.at[h], zero=peer).start()
+    mine = maxima.at[0, zero]
+    for peer in peers:
+        remote(mine, mine, max_send.at[0], max_recv.at[0], zero=peer).start()
+    mine = maxima.at[1, zero]
+    for peer in peers[0:-1:2]:
+        remote(mine, mine, max_send.at[1], max_recv.at[1], zero=peer).start()
+
+    right, left = shard_of(1), shard_of(-1)
+    starts = [sum(PIECES[:k]) for k in range(len(PIECES) + 1)]
+
+    def first_rows(way):
+        return remote(
+            w.at[pl.ds(0, EARLY)], early.at[way], early_send.at[0],
+            ring_recv.at[number[way, 0, 0]], zero=(right, left)[way],
+        )
+
+    @pl.when(core == 0)
+    def _():
+        first_rows(0).start()
+        first_rows(1).start()
+
     for peer in peers:
         mine = parts.at[zero]
         remote(mine, mine, part_send.at[0], part_recv.at[0], zero=peer).start()
 
-    right, left = shard_of(1), shard_of(-1)
-
     def piece(shard, k):
         return out.at[
-            pl.ds(k * chunk, chunk), pl.ds(pl.multiple_of(shard * LANES, LANES), LANES)
+            pl.ds(starts[k] * LANES, PIECES[k] * LANES),
+            pl.ds(pl.multiple_of(shard * LANES, LANES), LANES),
         ]
 
     def hop(way, step, shard, k):
         at = piece(shard, k)
+        sem = early_send if step == 0 and k == 0 else ring_send
         return remote(
-            at, at, ring_send.at[0], ring_recv.at[way, step, k], zero=(right, left)[way]
+            at, at, sem.at[0], ring_recv.at[number[way, step, k]], zero=(right, left)[way]
         )
 
     def pair(shard, k):
         at = piece(shard, k)
         return remote(at, at, pair_send.at[0], pair_recv.at[0], zero=partner)
 
-    def divide(k):
-        for j in range(k * blocks // CHUNKS, (k + 1) * blocks // CHUNKS):
+    def divide(k, shard=zero, source=w):
+        for j in range(starts[k], starts[k + 1]):
             at = pl.ds(j * LANES, LANES)
             by = jnp.broadcast_to(rows[j : j + 1, :], (LANES, LANES)).T
-            to = pl.ds(pl.multiple_of(zero * LANES, LANES), LANES)
-            out[at, to] = (w[at, :] / by).astype(jnp.bfloat16)
-
-    for h in (0, 1):
-        others = maxima.at[h, pl.ds(0, zeros - 1)]
-        remote(others, others, max_send.at[h], max_recv.at[h], zero=partner).wait_recv()
-        most = maxima[h, 0]
-        for i in range(1, zeros):
-            most = jnp.maximum(most, maxima[h, i])
-        rows[h * half_blocks : (h + 1) * half_blocks, :] = most
-        first, second = 2 * h, 2 * h + 1
-        divide(first)
-        hop(0, 0, zero, first).start()
-        divide(second)
-        hop(1, 0, zero, second).start()
-        hop(0, 0, zero, second).start()
-        hop(1, 0, zero, first).start()
-        pair(zero, first).start()
-        pair(zero, second).start()
+            to = pl.ds(pl.multiple_of(shard * LANES, LANES), LANES)
+            out[at, to] = (source[at, :] / by).astype(jnp.bfloat16)
+
+    others = maxima.at[0, pl.ds(0, zeros - 1)]
+    remote(others, others, max_send.at[0], max_recv.at[0], zero=partner).wait_recv()
+    most = maxima[0, 0]
+    for i in range(1, zeros):
+        most = jnp.maximum(most, maxima[0, i])
+    rows[0:half_blocks, :] = most
+
+    @pl.when(core == 1)
+    def _():
+        divide(0)
+        hop(0, 0, zero, 0).start()
+        hop(1, 0, zero, 0).start()
+
+    divide(1)
+    hop(0, 0, zero, 1).start()
+    hop(1, 0, zero, 1).start()
+    divide(2)
+    hop(0, 0, zero, 2).start()
+
+    others = maxima.at[1, pl.ds(0, chips - 1)]
+    remote(others, others, max_send.at[1], max_recv.at[1], zero=partner).wait_recv()
+    most = maxima[1, core]
+    for i in range(1, chips):
+        most = jnp.maximum(most, maxima[1, 2 * i + core])
+    shared[core] = most
+    ours = shared.at[core]
+    share_max = remote(ours, ours, pair_send.at[1], pair_recv.at[1], zero=partner)
+    share_max.start()
+
+    @pl.when(core == 0)
+    def _():
+        divide(0)
+
+    for k in (0, 1, 2):
+        pair(zero, k).start()
+    share_max.wait_recv()
+    rows[half_blocks:blocks, :] = jnp.maximum(shared[0], shared[1])
+    divide(3)
+    hop(0, 0, zero, 3).start()
+    hop(1, 0, zero, 3).start()
+    divide(4)
+    hop(0, 0, zero, 4).start()
+    hop(1, 0, zero, 4).start()
+    hop(1, 0, zero, 2).start()
+    for k in (3, 4):
+        pair(zero, k).start()
 
     per_expert = blocks // scale.shape[0]
     for j in range(blocks):
@@ -197,35 +259,60 @@
                 pl.ds(i, 2 * banks, stride=zeros), :
             ].astype(jnp.bfloat16)
 
-    stages = [x_second] + [functools.partial(y_step, step) for step in range(ups + 1)]
+    stages = [x_first, x_second] + [functools.partial(y_step, step) for step in range(ups + 1)]
 
     def forward(way, step, k, onward):
         shard = shard_of(-step if way == 0 else step)
-        hop(way, step - 1, shard, k).wait_recv()
+        if step == 1 and k == 0:
+
+            @pl.when(core == 0)
+            def _():
+                first_rows(way).wait_recv()
+                divide(0, shard, early.at[way])
+
+            @pl.when(core == 1)
+            def _():
+                hop(way, 0, shard, 0).wait_recv()
+        else:
+            hop(way, step - 1, shard, k).wait_recv()
         if onward:
             hop(way, step, shard, k).start()
         pair(shard, k).start()
 
-    x_first()
+    turn = 0
     for step in range(1, far):
-        for i in range(CHUNKS):
+        for i in range(len(PIECES)):
             for way in (0, 1):
                 k = ORDER[way][i]
                 forward(way, step, k, step < far - 1 or k in ONWARD[way])
-            if i % 2 == 1 and stages:
+            if turn % 2 == 1 and stages:
                 stages.pop(0)()
+            turn += 1
     for stage in stages:
         stage()
     finish_router()
-    for i in range(CHUNKS // 2):
+    for i in range(len(PIECES)):
         for way in (0, 1):
-            forward(way, far, ONWARD[way][i], False)
-
-    sent = out.at[:, pl.ds(0, (chips - 1) * LANES)]
-    remote(sent, sent, ring_send.at[0], ring_recv.at[0, 0, 0], zero=right).wait_send()
-    for h in (0, 1):
-        others = maxima.at[h, pl.ds(0, zeros - 1)]
+            if ORDER[way][i] in ONWARD[way]:
+                forward(way, far, ORDER[way][i], False)
+
+    size = (blocks * (chips - 1) - 2 * PIECES[0]) * LANES // chips
+    sent = out.at[pl.ds(0, size), pl.ds(0, chips * LANES)]
+    remote(sent, sent, ring_send.at[0], pair_recv.at[0], zero=right).wait_send()
+
+    @pl.when(core == 0)
+    def _():
+        remote(early, early, early_send.at[0], pair_recv.at[0], zero=right).wait_send()
+
+    @pl.when(core == 1)
+    def _():
+        sent = out.at[pl.ds(0, 2 * EARLY), pl.ds(0, LANES)]
+        remote(sent, sent, early_send.at[0], pair_recv.at[0], zero=right).wait_send()
+
+    for h, count in ((0, zeros - 1), (1, chips - 1)):
+        others = maxima.at[h, pl.ds(0, count)]
         remote(others, others, max_send.at[h], max_recv.at[h], zero=partner).wait_send()
+    share_max.wait_send()
     others = parts.at[pl.ds(0, zeros - 1)]
     remote(others, others, part_send.at[0], part_recv.at[0], zero=partner).wait_send()
     size = (ACROSS - 1 + (down - 1) * ACROSS) * 2 * zeros
@@ -269,11 +356,13 @@
             pltpu.VMEM((total, LANES), jnp.float32),
             pltpu.VMEM((2, LANES), jnp.float32),
             pltpu.VMEM((1, LANES), jnp.float32),
+            pltpu.VMEM((2, EARLY, LANES), jnp.float32),
             pltpu.VMEM((2, zeros, total // LANES // 2, LANES), jnp.float32),
+            pltpu.VMEM((2, total // LANES // 2, LANES), jnp.float32),
             pltpu.VMEM((total // LANES, LANES), jnp.float32),
             pltpu.VMEM((zeros, 1, 2 * LANES), jnp.float32),
             pltpu.VMEM((2 * banks * zeros, LANES), jnp.float32),
-            dma((CHUNKS + 2,)),
+            dma((LOADS + 2,)),
             dma((2,)),
             dma((2,)),
             dma((1,)),
@@ -282,9 +371,10 @@
             dma((ACROSS,)),
             dma((banks // ACROSS,)),
             dma((1,)),
-            dma((2, chips // 2, CHUNKS)),
             dma((1,)),
-            dma((1,)),
+            dma((len(arrivals(chips)),)),
+            dma((2,)),
+            dma((2,)),
         ],
         compiler_params=pltpu.CompilerParams(
             collective_id=0, has_side_effects=True, vmem_limit_bytes=24 * 1024 * 1024

time: 65.3 us -> 63.8 us (0.977)
  Pallas kernels: 64.5 us -> 63 us
    pallas_call x1, Pallas kernels: 61.1 us -> 59.6 us  [per_device(): pl.pallas_call(functools.partial(kernel, banks, zeros), out_shape=(jax.Sh...]
where the time goes in v3:
time: 63.8 us; the launch traced here: 63.7 us
  Pallas kernels  63 us (99%)
  between operations  0.64 us (1%)
    pallas_call x1, Pallas kernels, per_device(): pl.pallas_call(functools.partial(kernel, banks, zeros), out_shape=(jax.Sh...  59.6 us
    pallas_call x1, Pallas kernels, per_device(): pl.pallas_call(put_out, out_shape=tuple((jax.ShapeDtypeStruct(a.shape, a....  3.44 us

profile of v3, /device:TPU:1, one launch (start us, length us, event | category | flops | bytes accessed | tf_op | source)
XLA Modules:
  0.0 63.7 jit_solution(14594602577830827801)
XLA Ops:
  0.6 59.6 %shard_map.58 = (bf16[2048,2048]{1,0:T(8,128)(2,1)S(1)}, f32[2,1024]{1,0:T(2,128)S(1)}, bf16[64,2048]{1,0:T(8,128)(2,1)S(1)}) custom-call(f32[2048,128]{1,0:T(8,128)} %bitcast.5, f32[2,128]{1,0:T(2,128)} %bitcast.6, f32[1,128]{1,0:T(1,128)} %bitcast.7), custom_call_target="tpu_custom_call" | custom-call | tf_op jit(solution)/shard_map/pallas_call | solution.py:346
  60.2 3.4 %shard_map.59 = (bf16[2048,2048]{1,0:T(8,128)(2,1)}, f32[2,1024]{1,0:T(2,128)}, bf16[64,2048]{1,0:T(8,128)(2,1)}) custom-call(bf16[2048,2048]{1,0:T(8,128)(2,1)S(1)} %get-tuple-element.9.final, f32[2,1024]{1,0:T(2,128)S(1)} %get-tuple-element.10.scale, bf16[64,2048]{1,0:T(8,128)(2,1)S(1)} %get-tuple-element.11.router), custom_call_target="tpu_custom_call" | custom-call | tf_op jit(solution)/shard_map/pallas_call | solution.py:392

commit v4 on v3

--- a/solution.py
+++ b/solution.py
@@ -12,10 +12,12 @@
 ACROSS = 4
 LOADS = 4
 PUTS = 8
-PIECES = (4, 2, 2, 4, 4)
-EARLY = PIECES[0] * LANES
-ORDER = ((0, 1, 2, 3, 4), (0, 1, 3, 4, 2))
-ONWARD = ((0, 1, 2), (3, 4))
+PIECES = (4, 4, 6, 2)
+AHEAD = 2
+EARLY = PIECES[AHEAD] * LANES
+ORDER = ((0, 1, 2, 3), (0, 2, 3, 1))
+ONWARD = ((0, 1), (2, 3))
+TURNS = (0, 2, 4, 5, 7, 8, 10)
 
 
 def arrivals(chips):
@@ -33,7 +35,7 @@
     banks, zeros, w_hbm, r_hbm, g_hbm, out, scale, router,
     w, r, g, early, maxima, shared, rows, parts, columns,
     load_sem, max_send, max_recv, part_send, part_recv, col_send, x_recv, y_recv,
-    early_send, ring_send, ring_recv, pair_send, pair_recv,
+    early_send, ring_send, ring_recv, pair_send, pair_recv, hello,
 ):
     total = w_hbm.shape[0]
     blocks = total // LANES
@@ -79,11 +81,52 @@
         load(i).start()
     load_r.start()
     load_g.start()
-    beside = [along_x(1), along_x(-1), along_y(1) * ACROSS + x]
-    if down > 2:
-        beside.append(along_y(-1) * ACROSS + x)
-    for peer in beside:
-        pl.semaphore_signal(barrier, inc=1, device_id={"bank": peer}, device_id_type=MESH)
+
+    sides = (
+        (x, ACROSS, lambda to: to + y * ACROSS, hello.at[0]),
+        (y, down, lambda to: to * ACROSS + x, hello.at[1]),
+    )
+
+    def to_higher(here, size, bank_of, signal):
+        @pl.when(here < size - 1)
+        def _():
+            signal(bank_of(here + 1))
+
+        if size > 2:
+
+            @pl.when(here == 0)
+            def _():
+                signal(bank_of(size - 1))
+
+    def to_lower(here, size, bank_of, signal):
+        @pl.when(here > 0)
+        def _():
+            signal(bank_of(here - 1))
+
+        if size > 2:
+
+            @pl.when(here == size - 1)
+            def _():
+                signal(bank_of(0))
+
+    def lower(here, size):
+        return (here + size - 1) // size + ((here + 1) // size if size > 2 else 0)
+
+    def higher(here, size):
+        return (2 if size > 2 else 1) - lower(here, size)
+
+    def answers(here, size, sem):
+        @pl.when(higher(here, size) > 0)
+        def _():
+            pl.semaphore_wait(sem, higher(here, size))
+
+    for here, size, bank_of, _ in sides:
+        to_higher(
+            here, size, bank_of,
+            lambda to: pl.semaphore_signal(
+                barrier, inc=1, device_id={"bank": to}, device_id_type=MESH
+            ),
+        )
 
     for i in range(LOADS):
         load(i).wait()
@@ -97,7 +140,7 @@
     parts[zero, :, 0:LANES] = product[0:1]
     parts[zero, :, LANES : 2 * LANES] = product[1:2]
 
-    pl.semaphore_wait(barrier, zeros - 1 + len(beside))
+    pl.semaphore_wait(barrier, zeros - 1 + lower(x, ACROSS) + lower(y, down))
 
     mine = maxima.at[0, zero]
     for peer in peers:
@@ -111,8 +154,8 @@
 
     def first_rows(way):
         return remote(
-            w.at[pl.ds(0, EARLY)], early.at[way], early_send.at[0],
-            ring_recv.at[number[way, 0, 0]], zero=(right, left)[way],
+            w.at[pl.ds(starts[AHEAD] * LANES, EARLY)], early.at[way], early_send.at[0],
+            ring_recv.at[number[way, 0, AHEAD]], zero=(right, left)[way],
         )
 
     @pl.when(core == 0)
@@ -123,6 +166,13 @@
     for peer in peers:
         mine = parts.at[zero]
         remote(mine, mine, part_send.at[0], part_recv.at[0], zero=peer).start()
+    for here, size, bank_of, sem in sides:
+        to_lower(
+            here, size, bank_of,
+            lambda to: pl.semaphore_signal(
+                sem, inc=1, device_id={"bank": to}, device_id_type=MESH
+            ),
+        )
 
     def piece(shard, k):
         return out.at[
@@ -132,7 +182,7 @@
 
     def hop(way, step, shard, k):
         at = piece(shard, k)
-        sem = early_send if step == 0 and k == 0 else ring_send
+        sem = early_send if step == 0 and k == AHEAD else ring_send
         return remote(
             at, at, sem.at[0], ring_recv.at[number[way, step, k]], zero=(right, left)[way]
         )
@@ -141,12 +191,12 @@
         at = piece(shard, k)
         return remote(at, at, pair_send.at[0], pair_recv.at[0], zero=partner)
 
-    def divide(k, shard=zero, source=w):
+    def divide(k, shard=zero, source=w, first=0):
         for j in range(starts[k], starts[k + 1]):
-            at = pl.ds(j * LANES, LANES)
+            at, source_at = pl.ds(j * LANES, LANES), pl.ds((j - first) * LANES, LANES)
             by = jnp.broadcast_to(rows[j : j + 1, :], (LANES, LANES)).T
             to = pl.ds(pl.multiple_of(shard * LANES, LANES), LANES)
-            out[at, to] = (source[at, :] / by).astype(jnp.bfloat16)
+            out[at, to] = (source[source_at, :] / by).astype(jnp.bfloat16)
 
     others = maxima.at[0, pl.ds(0, zeros - 1)]
     remote(others, others, max_send.at[0], max_recv.at[0], zero=partner).wait_recv()
@@ -155,17 +205,11 @@
         most = jnp.maximum(most, maxima[0, i])
     rows[0:half_blocks, :] = most
 
-    @pl.when(core == 1)
-    def _():
-        divide(0)
-        hop(0, 0, zero, 0).start()
-        hop(1, 0, zero, 0).start()
-
+    divide(0)
+    hop(0, 0, zero, 0).start()
+    hop(1, 0, zero, 0).start()
     divide(1)
     hop(0, 0, zero, 1).start()
-    hop(1, 0, zero, 1).start()
-    divide(2)
-    hop(0, 0, zero, 2).start()
 
     others = maxima.at[1, pl.ds(0, chips - 1)]
     remote(others, others, max_send.at[1], max_recv.at[1], zero=partner).wait_recv()
@@ -177,22 +221,20 @@
     share_max = remote(ours, ours, pair_send.at[1], pair_recv.at[1], zero=partner)
     share_max.start()
 
-    @pl.when(core == 0)
-    def _():
-        divide(0)
-
-    for k in (0, 1, 2):
-        pair(zero, k).start()
     share_max.wait_recv()
     rows[half_blocks:blocks, :] = jnp.maximum(shared[0], shared[1])
+    divide(AHEAD)
+
+    @pl.when(core == 1)
+    def _():
+        hop(1, 0, zero, AHEAD).start()
+        hop(0, 0, zero, AHEAD).start()
+
     divide(3)
+    hop(1, 0, zero, 3).start()
     hop(0, 0, zero, 3).start()
-    hop(1, 0, zero, 3).start()
-    divide(4)
-    hop(0, 0, zero, 4).start()
-    hop(1, 0, zero, 4).start()
-    hop(1, 0, zero, 2).start()
-    for k in (3, 4):
+    hop(1, 0, zero, 1).start()
+    for k in range(len(PIECES)):
         pair(zero, k).start()
 
     per_expert = blocks // scale.shape[0]
@@ -206,13 +248,7 @@
 
     def send_x(distance, peer):
         at = banks_of(along_x(distance), 1)
-        return remote(at, at, col_send.at[0], x_recv.at[distance % ACROSS], bank=peer)
-
-    def send_y(distance, peer):
-        at = banks_of(along_y(distance) * ACROSS, ACROSS)
-        return remote(
-            at, at, col_send.at[0], y_recv.at[distance % down], bank=peer * ACROSS + x
-        )
+        return remote(at, at, col_send.at[0], x_recv.at[abs(distance) - 1], bank=peer)
 
     def x_first():
         others = parts.at[pl.ds(0, zeros - 1)]
@@ -221,35 +257,38 @@
         for i in range(zeros):
             columns[pl.ds(tile + i, 1), :] = parts[i, :, 0:LANES]
             columns[pl.ds(tile + zeros + i, 1), :] = parts[i, :, LANES : 2 * LANES]
+        answers(x, ACROSS, hello.at[0])
         at = banks_of(bank, 1)
-        remote(at, at, col_send.at[0], x_recv.at[ACROSS - 1], bank=along_x(1)).start()
-        remote(at, at, col_send.at[0], x_recv.at[1], bank=along_x(-1)).start()
+        remote(at, at, col_send.at[0], x_recv.at[0], bank=along_x(1)).start()
+        remote(at, at, col_send.at[0], x_recv.at[0], bank=along_x(-1)).start()
 
     def x_second():
-        send_x(-1, along_x(1)).wait_recv()
-        send_x(1, along_x(-1)).wait_recv()
+        both = banks_of(0, 2)
+        remote(both, both, col_send.at[0], x_recv.at[0], bank=along_x(1)).wait_recv()
         at = banks_of(along_x(-1), 1)
-        remote(at, at, col_send.at[0], x_recv.at[2], bank=along_x(1)).start()
+        remote(at, at, col_send.at[0], x_recv.at[1], bank=along_x(1)).start()
 
     ups, downs = down // 2, (down - 1) // 2
 
     def y_step(step):
         if step == 0:
             send_x(2, along_x(1)).wait_recv()
+            answers(y, down, hello.at[1])
         if 1 <= step <= ups:
-            send_y(-step, along_y(1)).wait_recv()
-        if 1 <= step <= downs:
-            send_y(step, along_y(-1)).wait_recv()
+            came = banks_of(0, (2 if step <= downs else 1) * ACROSS)
+            remote(
+                came, came, col_send.at[0], y_recv.at[step - 1], bank=along_x(1)
+            ).wait_recv()
         if step < ups:
             at = banks_of(along_y(-step) * ACROSS, ACROSS)
             remote(
-                at, at, col_send.at[0], y_recv.at[(-step - 1) % down],
+                at, at, col_send.at[0], y_recv.at[step],
                 bank=along_y(1) * ACROSS + x,
             ).start()
         if step < downs:
             at = banks_of(along_y(step) * ACROSS, ACROSS)
             remote(
-                at, at, col_send.at[0], y_recv.at[(step + 1) % down],
+                at, at, col_send.at[0], y_recv.at[step],
                 bank=along_y(-1) * ACROSS + x,
             ).start()
 
@@ -263,16 +302,16 @@
 
     def forward(way, step, k, onward):
         shard = shard_of(-step if way == 0 else step)
-        if step == 1 and k == 0:
+        if step == 1 and k == AHEAD:
 
             @pl.when(core == 0)
             def _():
                 first_rows(way).wait_recv()
-                divide(0, shard, early.at[way])
+                divide(k, shard, early.at[way], starts[k])
 
             @pl.when(core == 1)
             def _():
-                hop(way, 0, shard, 0).wait_recv()
+                hop(way, 0, shard, k).wait_recv()
         else:
             hop(way, step - 1, shard, k).wait_recv()
         if onward:
@@ -285,18 +324,17 @@
             for way in (0, 1):
                 k = ORDER[way][i]
                 forward(way, step, k, step < far - 1 or k in ONWARD[way])
-            if turn % 2 == 1 and stages:
+            if turn in TURNS and stages:
                 stages.pop(0)()
             turn += 1
     for stage in stages:
         stage()
     finish_router()
-    for i in range(len(PIECES)):
+    for i in range(len(ONWARD[0])):
         for way in (0, 1):
-            if ORDER[way][i] in ONWARD[way]:
-                forward(way, far, ORDER[way][i], False)
-
-    size = (blocks * (chips - 1) - 2 * PIECES[0]) * LANES // chips
+            forward(way, far, ONWARD[way][i], False)
+
+    size = ((chips - 1) * total - 2 * EARLY) // chips
     sent = out.at[pl.ds(0, size), pl.ds(0, chips * LANES)]
     remote(sent, sent, ring_send.at[0], pair_recv.at[0], zero=right).wait_send()
 
@@ -368,13 +406,14 @@
             dma((1,)),
             dma((1,)),
             dma((1,)),
-            dma((ACROSS,)),
-            dma((banks // ACROSS,)),
+            dma((ACROSS // 2,)),
+            dma((banks // ACROSS // 2,)),
             dma((1,)),
             dma((1,)),
             dma((len(arrivals(chips)),)),
             dma((2,)),
             dma((2,)),
+            pltpu.SemaphoreType.REGULAR((2,)),
         ],
         compiler_params=pltpu.CompilerParams(
             collective_id=0, has_side_effects=True, vmem_limit_bytes=24 * 1024 * 1024

time: 63.8 us -> 62.6 us (0.981)
  Pallas kernels: 63 us -> 61.8 us
    pallas_call x1, Pallas kernels: 59.6 us -> 58.4 us  [per_device(): pl.pallas_call(functools.partial(kernel, banks, zeros), out_shape=(jax.Sh...]
where the time goes in v4:
time: 62.6 us; the launch traced here: 62.5 us
  Pallas kernels  61.8 us (99%)
  between operations  0.64 us (1%)
    pallas_call x1, Pallas kernels, per_device(): pl.pallas_call(functools.partial(kernel, banks, zeros), out_shape=(jax.Sh...  58.4 us
    pallas_call x1, Pallas kernels, per_device(): pl.pallas_call(put_out, out_shape=tuple((jax.ShapeDtypeStruct(a.shape, a....  3.44 us

profile of v4, /device:TPU:1, one launch (start us, length us, event | category | flops | bytes accessed | tf_op | source)
XLA Modules:
  0.0 62.5 jit_solution(12044613598305598637)
XLA Ops:
  0.6 58.4 %shard_map.58 = (bf16[2048,2048]{1,0:T(8,128)(2,1)S(1)}, f32[2,1024]{1,0:T(2,128)S(1)}, bf16[64,2048]{1,0:T(8,128)(2,1)S(1)}) custom-call(f32[2048,128]{1,0:T(8,128)} %bitcast.5, f32[2,128]{1,0:T(2,128)} %bitcast.6, f32[1,128]{1,0:T(1,128)} %bitcast.7), custom_call_target="tpu_custom_call" | custom-call | tf_op jit(solution)/shard_map/pallas_call | solution.py:384
  59.0 3.4 %shard_map.59 = (bf16[2048,2048]{1,0:T(8,128)(2,1)}, f32[2,1024]{1,0:T(2,128)}, bf16[64,2048]{1,0:T(8,128)(2,1)}) custom-call(bf16[2048,2048]{1,0:T(8,128)(2,1)S(1)} %get-tuple-element.9.final, f32[2,1024]{1,0:T(2,128)S(1)} %get-tuple-element.10.scale, bf16[64,2048]{1,0:T(8,128)(2,1)S(1)} %get-tuple-element.11.router), custom_call_target="tpu_custom_call" | custom-call | tf_op jit(solution)/shard_map/pallas_call | solution.py:431

commit v5 on v4

--- a/solution.py
+++ b/solution.py
@@ -14,10 +14,11 @@
 PUTS = 8
 PIECES = (4, 4, 6, 2)
 AHEAD = 2
+QUARTER = PIECES[0]
 EARLY = PIECES[AHEAD] * LANES
 ORDER = ((0, 1, 2, 3), (0, 2, 3, 1))
 ONWARD = ((0, 1), (2, 3))
-TURNS = (0, 2, 4, 5, 7, 8, 10)
+TURNS = (1, 2, 3, 5, 7, 9, 11)
 
 
 def arrivals(chips):
@@ -33,13 +34,12 @@
 
 def kernel(
     banks, zeros, w_hbm, r_hbm, g_hbm, out, scale, router,
-    w, r, g, early, maxima, shared, rows, parts, columns,
+    w, r, g, early, lead, rest, shared, rows, parts, columns,
     load_sem, max_send, max_recv, part_send, part_recv, col_send, x_recv, y_recv,
     early_send, ring_send, ring_recv, pair_send, pair_recv, hello,
 ):
     total = w_hbm.shape[0]
     blocks = total // LANES
-    half_blocks = blocks // 2
     chips, down = zeros // 2, banks // ACROSS
     far, number = chips // 2, arrivals(chips)
     bank, zero = lax.axis_index("bank"), lax.axis_index("zero")
@@ -132,8 +132,12 @@
         load(i).wait()
         for j in range(i * blocks // LOADS, (i + 1) * blocks // LOADS):
             block = jnp.abs(w[j * LANES : (j + 1) * LANES, :])
-            h, k = j // half_blocks, j % half_blocks
-            maxima[h, zero, k : k + 1, :] = jnp.max(block.T, axis=0, keepdims=True)
+            q, k = j // QUARTER, j % QUARTER
+            row = jnp.max(block.T, axis=0, keepdims=True)
+            if q == 0:
+                lead[zero, k : k + 1, :] = row
+            else:
+                rest[zero, q - 1, k : k + 1, :] = row
     load_r.wait()
     load_g.wait()
     product = r[...] * g[...]
@@ -142,10 +146,10 @@
 
     pl.semaphore_wait(barrier, zeros - 1 + lower(x, ACROSS) + lower(y, down))
 
-    mine = maxima.at[0, zero]
+    mine = lead.at[zero]
     for peer in peers:
         remote(mine, mine, max_send.at[0], max_recv.at[0], zero=peer).start()
-    mine = maxima.at[1, zero]
+    mine = rest.at[zero]
     for peer in peers[0:-1:2]:
         remote(mine, mine, max_send.at[1], max_recv.at[1], zero=peer).start()
 
@@ -198,31 +202,32 @@
             to = pl.ds(pl.multiple_of(shard * LANES, LANES), LANES)
             out[at, to] = (source[source_at, :] / by).astype(jnp.bfloat16)
 
-    others = maxima.at[0, pl.ds(0, zeros - 1)]
+    others = lead.at[pl.ds(0, zeros - 1)]
     remote(others, others, max_send.at[0], max_recv.at[0], zero=partner).wait_recv()
-    most = maxima[0, 0]
+    most = lead[0]
     for i in range(1, zeros):
-        most = jnp.maximum(most, maxima[0, i])
-    rows[0:half_blocks, :] = most
-
+        most = jnp.maximum(most, lead[i])
+    rows[0:QUARTER, :] = most
     divide(0)
     hop(0, 0, zero, 0).start()
     hop(1, 0, zero, 0).start()
-    divide(1)
-    hop(0, 0, zero, 1).start()
-
-    others = maxima.at[1, pl.ds(0, chips - 1)]
+
+    others = rest.at[pl.ds(0, chips - 1)]
     remote(others, others, max_send.at[1], max_recv.at[1], zero=partner).wait_recv()
-    most = maxima[1, core]
+    most = rest[core]
     for i in range(1, chips):
-        most = jnp.maximum(most, maxima[1, 2 * i + core])
+        most = jnp.maximum(most, rest[2 * i + core])
     shared[core] = most
     ours = shared.at[core]
     share_max = remote(ours, ours, pair_send.at[1], pair_recv.at[1], zero=partner)
     share_max.start()
-
     share_max.wait_recv()
-    rows[half_blocks:blocks, :] = jnp.maximum(shared[0], shared[1])
+    for q in range(1, blocks // QUARTER):
+        rows[q * QUARTER : (q + 1) * QUARTER, :] = jnp.maximum(
+            shared[0, q - 1], shared[1, q - 1]
+        )
+    divide(1)
+    hop(0, 0, zero, 1).start()
     divide(AHEAD)
 
     @pl.when(core == 1)
@@ -302,28 +307,32 @@
 
     def forward(way, step, k, onward):
         shard = shard_of(-step if way == 0 else step)
-        if step == 1 and k == AHEAD:
-
-            @pl.when(core == 0)
-            def _():
-                first_rows(way).wait_recv()
-                divide(k, shard, early.at[way], starts[k])
-
-            @pl.when(core == 1)
-            def _():
-                hop(way, 0, shard, k).wait_recv()
-        else:
-            hop(way, step - 1, shard, k).wait_recv()
+        hop(way, step - 1, shard, k).wait_recv()
         if onward:
             hop(way, step, shard, k).start()
         pair(shard, k).start()
+
+    def forward_early(way):
+        shard = shard_of(-1 if way == 0 else 1)
+        first_rows(way).wait_recv()
+        divide(AHEAD, shard, early.at[way], starts[AHEAD])
+        hop(way, 1, shard, AHEAD).start()
+        pair(shard, AHEAD).start()
+
+    @pl.when(core == 0)
+    def _():
+        forward_early(0)
+        forward_early(1)
 
     turn = 0
     for step in range(1, far):
         for i in range(len(PIECES)):
             for way in (0, 1):
                 k = ORDER[way][i]
-                forward(way, step, k, step < far - 1 or k in ONWARD[way])
+                if step == 1 and k == AHEAD:
+                    pl.when(core == 1)(functools.partial(forward, way, step, k, True))
+                else:
+                    forward(way, step, k, step < far - 1 or k in ONWARD[way])
             if turn in TURNS and stages:
                 stages.pop(0)()
             turn += 1
@@ -347,9 +356,10 @@
         sent = out.at[pl.ds(0, 2 * EARLY), pl.ds(0, LANES)]
         remote(sent, sent, early_send.at[0], pair_recv.at[0], zero=right).wait_send()
 
-    for h, count in ((0, zeros - 1), (1, chips - 1)):
-        others = maxima.at[h, pl.ds(0, count)]
-        remote(others, others, max_send.at[h], max_recv.at[h], zero=partner).wait_send()
+    others = lead.at[pl.ds(0, zeros - 1)]
+    remote(others, others, max_send.at[0], max_recv.at[0], zero=partner).wait_send()
+    others = rest.at[pl.ds(0, chips - 1)]
+    remote(others, others, max_send.at[1], max_recv.at[1], zero=partner).wait_send()
     share_max.wait_send()
     others = parts.at[pl.ds(0, zeros - 1)]
     remote(others, others, part_send.at[0], part_recv.at[0], zero=partner).wait_send()
@@ -379,7 +389,7 @@
 def per_device(banks, zeros, master_down, router_weight, router_gain):
     experts, inner, width = master_down.shape
     total = experts * inner
-    chips = zeros // 2
+    chips, quarters = zeros // 2, total // LANES // QUARTER
     dma = pltpu.SemaphoreType.DMA
     final, scale, router = pl.pallas_call(
         functools.partial(kernel, banks, zeros),
@@ -395,8 +405,9 @@
             pltpu.VMEM((2, LANES), jnp.float32),
             pltpu.VMEM((1, LANES), jnp.float32),
             pltpu.VMEM((2, EARLY, LANES), jnp.float32),
-            pltpu.VMEM((2, zeros, total // LANES // 2, LANES), jnp.float32),
-            pltpu.VMEM((2, total // LANES // 2, LANES), jnp.float32),
+            pltpu.VMEM((zeros, QUARTER, LANES), jnp.float32),
+            pltpu.VMEM((zeros, quarters - 1, QUARTER, LANES), jnp.float32),
+            pltpu.VMEM((2, quarters - 1, QUARTER, LANES), jnp.float32),
             pltpu.VMEM((total // LANES, LANES), jnp.float32),
             pltpu.VMEM((zeros, 1, 2 * LANES), jnp.float32),
             pltpu.VMEM((2 * banks * zeros, LANES), jnp.float32),

time: 62.6 us -> 62.4 us (level)
  no operation moved by 1% of the time
where the time goes in v5:
time: 62.4 us; the launch traced here: 62.3 us
  Pallas kernels  61.6 us (99%)
  between operations  0.64 us (1%)
    pallas_call x1, Pallas kernels, per_device(): pl.pallas_call(functools.partial(kernel, banks, zeros), out_shape=(jax.Sh...  58.2 us
    pallas_call x1, Pallas kernels, per_device(): pl.pallas_call(put_out, out_shape=tuple((jax.ShapeDtypeStruct(a.shape, a....  3.44 us

profile of v5, /device:TPU:1, one launch (start us, length us, event | category | flops | bytes accessed | tf_op | source)
XLA Modules:
  0.0 62.3 jit_solution(2637273896801441533)
XLA Ops:
  0.6 58.2 %shard_map.58 = (bf16[2048,2048]{1,0:T(8,128)(2,1)S(1)}, f32[2,1024]{1,0:T(2,128)S(1)}, bf16[64,2048]{1,0:T(8,128)(2,1)S(1)}) custom-call(f32[2048,128]{1,0:T(8,128)} %bitcast.5, f32[2,128]{1,0:T(2,128)} %bitcast.6, f32[1,128]{1,0:T(1,128)} %bitcast.7), custom_call_target="tpu_custom_call" | custom-call | tf_op jit(solution)/shard_map/pallas_call | solution.py:394
  58.8 3.4 %shard_map.59 = (bf16[2048,2048]{1,0:T(8,128)(2,1)}, f32[2,1024]{1,0:T(2,128)}, bf16[64,2048]{1,0:T(8,128)(2,1)}) custom-call(bf16[2048,2048]{1,0:T(8,128)(2,1)S(1)} %get-tuple-element.9.final, f32[2,1024]{1,0:T(2,128)S(1)} %get-tuple-element.10.scale, bf16[64,2048]{1,0:T(8,128)(2,1)S(1)} %get-tuple-element.11.router), custom_call_target="tpu_custom_call" | custom-call | tf_op jit(solution)/shard_map/pallas_call | solution.py:442

commit v6 on v5

--- a/solution.py
+++ b/solution.py
@@ -18,7 +18,7 @@
 EARLY = PIECES[AHEAD] * LANES
 ORDER = ((0, 1, 2, 3), (0, 2, 3, 1))
 ONWARD = ((0, 1), (2, 3))
-TURNS = (1, 2, 3, 5, 7, 9, 11)
+TURNS = (1, 3, 4, 6, 8, 9, 11)
 
 
 def arrivals(chips):

time: 62.4 us -> 62.4 us (level)
  no operation moved by 1% of the time
where the time goes in v6:
time: 62.4 us; the launch traced here: 62.3 us
  Pallas kernels  61.6 us (99%)
  between operations  0.64 us (1%)
    pallas_call x1, Pallas kernels, per_device(): pl.pallas_call(functools.partial(kernel, banks, zeros), out_shape=(jax.Sh...  58.2 us
    pallas_call x1, Pallas kernels, per_device(): pl.pallas_call(put_out, out_shape=tuple((jax.ShapeDtypeStruct(a.shape, a....  3.44 us

profile of v6, /device:TPU:1, one launch (start us, length us, event | category | flops | bytes accessed | tf_op | source)
XLA Modules:
  0.0 62.3 jit_solution(2609421326365797516)
XLA Ops:
  0.6 58.2 %shard_map.58 = (bf16[2048,2048]{1,0:T(8,128)(2,1)S(1)}, f32[2,1024]{1,0:T(2,128)S(1)}, bf16[64,2048]{1,0:T(8,128)(2,1)S(1)}) custom-call(f32[2048,128]{1,0:T(8,128)} %bitcast.5, f32[2,128]{1,0:T(2,128)} %bitcast.6, f32[1,128]{1,0:T(1,128)} %bitcast.7), custom_call_target="tpu_custom_call" | custom-call | tf_op jit(solution)/shard_map/pallas_call | solution.py:394
  58.8 3.4 %shard_map.59 = (bf16[2048,2048]{1,0:T(8,128)(2,1)}, f32[2,1024]{1,0:T(2,128)}, bf16[64,2048]{1,0:T(8,128)(2,1)}) custom-call(bf16[2048,2048]{1,0:T(8,128)(2,1)S(1)} %get-tuple-element.9.final, f32[2,1024]{1,0:T(2,128)S(1)} %get-tuple-element.10.scale, bf16[64,2048]{1,0:T(8,128)(2,1)S(1)} %get-tuple-element.11.router), custom_call_target="tpu_custom_call" | custom-call | tf_op jit(solution)/shard_map/pallas_call | solution.py:442
